TPU v7x, 32 devices: a whole 2x2x4 slice. The times are simulated.
32 devices in a mesh: kv: 16 (over z, y, x), head: 2 (over core).
Axes of the slice: x: 2, y: 2, z: 4, core: 2. Of those that a mesh axis runs over, the one named last changes fastest.
Arguments:
- queries: bfloat16 [8, 256, 128], P('head', 'kv'), may hold values from -384 to 384
- key_cache: bfloat16 [4096, 8, 128, 128], P('kv', 'head'), may hold values from -6 to 6
- value_cache: bfloat16 [4096, 8, 128, 128], P('kv', 'head'), may hold values from -6 to 6
- key_new: bfloat16 [32, 8, 128], P(None, 'head'), may hold values from -6 to 6
- value_new: bfloat16 [32, 8, 128], P(None, 'head'), may hold values from -6 to 6
- lengths: int32 [32], replicated, may hold values from 2 to 16385, as said below
- page_table: int32 [4096], replicated, may hold values from 0 to 4095, each once
Outputs:
- attended: bfloat16 [8, 256, 128], P('head', 'kv')
Inputs may be any that keep to these rules, and one draw needn't show every extreme that they name: The cache holds the first lengths[s] - 1 tokens of sequence s; some sequence has the largest length. `page_table`: every page appears once; page g lies on kv index g // 256.
All inputs are finite; a program needn't handle non-finite values.
Results may differ from a plain program's by a relative error of at most 0.0025.
Values may be sent and summed in bfloat16 or wider, within the bound.
A program may use at most 128 MiB of HBM per device.

v0:
```python
import math
import jax
import jax.numpy as jnp
from jax import lax
from jax.sharding import PartitionSpec as P

LOWEST_SCORE = -1e30


def finish(cache_max, cache_sum, cache_out, query_wide, fresh_key, fresh_value, score_scale):
    new_score = jnp.sum(query_wide * fresh_key.astype(jnp.float32), axis=-1) * score_scale
    highest = jnp.maximum(cache_max, new_score)
    old_part = jnp.exp(cache_max - highest)
    new_part = jnp.exp(new_score - highest)
    numerator = cache_out * old_part[..., None] + new_part[..., None] * fresh_value.astype(
        jnp.float32
    )
    denominator = cache_sum * old_part + new_part
    return (numerator / denominator[..., None]).astype(jnp.bfloat16)


def fold_triples(pieces):
    piece_max, piece_sum, piece_out = pieces
    highest = jnp.max(piece_max, axis=0)
    factor = jnp.exp(piece_max - highest[None])
    return (
        highest,
        jnp.sum(piece_sum * factor, axis=0),
        jnp.sum(piece_out * factor[..., None], axis=0),
    )


def on_device(queries, key_cache, value_cache, key_new, value_new, lengths, page_table):
    all_query = lax.all_gather(queries, "kv", axis=1, tiled=True)
    seq_count = lengths.shape[0]
    page_total = page_table.shape[0]
    pages_here = key_cache.shape[0]
    kv_here = key_cache.shape[1]
    page_len = key_cache.shape[2]
    head_width = key_cache.shape[3]
    rows_all = all_query.shape[1]
    group_size = rows_all // seq_count
    page_slots = page_total // seq_count
    local_rows = queries.shape[1]
    score_scale = 1.0 / math.sqrt(head_width)
    kv_index = lax.axis_index("kv")
    inverse = (
        jnp.zeros((page_total,), jnp.int32)
        .at[page_table]
        .set(jnp.arange(page_total, dtype=jnp.int32))
    )
    local_ids = lax.dynamic_slice_in_dim(inverse, kv_index * pages_here, pages_here)
    page_seq = local_ids // page_slots
    page_slot = local_ids % page_slots
    grouped = all_query.reshape(kv_here, seq_count, group_size, head_width)
    page_query = grouped[:, page_seq]
    scores = (
        jnp.einsum("gpqd,pgtd->pgqt", page_query, key_cache, preferred_element_type=jnp.float32)
        * score_scale
    )
    positions = page_slot[:, None] * page_len + jnp.arange(page_len, dtype=jnp.int32)[None, :]
    in_cache = (positions < (lengths[page_seq] - 1)[:, None])[:, None, None, :]
    masked = jnp.where(in_cache, scores, LOWEST_SCORE)
    page_max = jnp.max(masked, axis=3)
    weights = jnp.where(in_cache, jnp.exp(masked - page_max[..., None]), 0.0)
    page_sum = jnp.sum(weights, axis=3)
    page_out = jnp.einsum(
        "pgqt,pgtd->pgqd",
        weights.astype(jnp.bfloat16),
        value_cache,
        preferred_element_type=jnp.float32,
    )
    member = page_seq[None, :] == jnp.arange(seq_count, dtype=jnp.int32)[:, None]
    seq_best = jnp.max(jnp.where(member[:, :, None, None], page_max[None], LOWEST_SCORE), axis=1)
    factor = jnp.exp(page_max - seq_best[page_seq])
    onehot = member.astype(jnp.float32)
    seq_sum = jnp.einsum("sp,pgq->gsq", onehot, page_sum * factor, precision=lax.Precision.HIGHEST)
    seq_out = jnp.einsum(
        "sp,pgqd->gsqd", onehot, page_out * factor[..., None], precision=lax.Precision.HIGHEST
    )
    seq_max = jnp.transpose(seq_best, (1, 0, 2)).reshape(kv_here, rows_all)
    seq_sum = seq_sum.reshape(kv_here, rows_all)
    seq_out = seq_out.reshape(kv_here, rows_all, head_width)
    cache_max, cache_sum, cache_out = fold_triples(
        (
            lax.all_to_all(seq_max[None], "kv", split_axis=2, concat_axis=0, tiled=True),
            lax.all_to_all(seq_sum[None], "kv", split_axis=2, concat_axis=0, tiled=True),
            lax.all_to_all(seq_out[None], "kv", split_axis=2, concat_axis=0, tiled=True),
        )
    )
    row_seq = (kv_index * local_rows + jnp.arange(local_rows, dtype=jnp.int32)) // group_size
    fresh_key = jnp.transpose(key_new[row_seq], (1, 0, 2))
    fresh_value = jnp.transpose(value_new[row_seq], (1, 0, 2))
    query_wide = queries.astype(jnp.float32)
    return finish(cache_max, cache_sum, cache_out, query_wide, fresh_key, fresh_value, score_scale)


def solution(mesh):
    placed = (
        P("head", "kv", None),
        P("kv", "head", None, None),
        P("kv", "head", None, None),
        P(None, "head", None),
        P(None, "head", None),
        P(),
        P(),
    )
    return jax.shard_map(
        on_device, mesh=mesh, in_specs=placed, out_specs=P("head", "kv", None), check_vma=False
    )
```

profile of v0, /device:TPU:0, one launch (start us, length us, event | category | flops | bytes accessed | tf_op | source)
XLA Modules:
  0.0 175.0 jit_solution(6055094217681499025)
XLA Ops:
  0.0 2.1 %fusion.45 = (s32[1]{0:T(128)}, s32[1]{0:T(128)}, s32[1]{0:T(128)}, s32[1]{0:T(128)}, s32[1]{0:T(128)}, /*index=5*/s32[1]{0:T(128)}, s32[1]{0:T(128)}, s32[1]{0:...) fusion(s32[32]{0:T(128)} %param.12), kind=kLoop, calls=%fused_computation.108 | loop fusion | bytes 152 | tf_op jit(solution)/shard_map/gather | solution.py:62
  2.1 1.8 %fusion.46 = (s32[1]{0:T(128)}, s32[1]{0:T(128)}, s32[1]{0:T(128)}, s32[1]{0:T(128)}, s32[1]{0:T(128)}, /*index=5*/s32[1]{0:T(128)}, s32[1]{0:T(128)}, s32[1]{0:...) fusion(s32[32]{0:T(128)} %param.12), kind=kLoop, calls=%fused_computation.109 | loop fusion | bytes 104 | tf_op jit(solution)/shard_map/gather | solution.py:62
  3.9 0.7 compare_select_fusion
  4.7 15.5 %scatter_custom_fusion = s32[4096]{0:T(1024)S(1)} fusion(s32[4096]{0:T(1024)S(1)} %compare_select_fusion, s32[4096]{0:T(1024)S(1)} %iota.23, s32[]{:T(128)} %constant.32.clone.1), kind=kCustom, calls=%fused_computation.48 | custom fusion | bytes 16388 | tf_op jit(solution)/shard_map/scatter | solution.py:50
  20.3 20.1 %fusion.36 = (s32[256]{0:T(256)S(1)}, s32[256]{0:T(256)S(1)}) fusion(s32[]{:T(128)} %bitcast, s32[]{:T(128)} %bitcast.1, s32[]{:T(128)} %bitcast.2, s32[]{:T(128)} %bitcast.3, s32[]{:T(128)} %bitcast.4, s32[]{:T(128)} %bitcast.5, s32[]{:T(128)} %bitcast.6, s32[]{:T(128)} %bitcast.7, s32[]{:T(128)} %bitcast.8, s32[]{:T(128)} %bitcast.9, s32[]{:T(128)} %bitcast.10, ...), kind=kLoop, calls=%fused_computation.100 | loop fusion | flops 20736 | bytes 3204 | tf_op jit(solution)/shard_map/sub | solution.py:62
  40.5 44.0 %all_gather.3 = bf16[4,256,128]{2,1,0:T(8,128)(2,1)S(1)} all-gather(bf16[4,16,128]{2,1,0:T(8,128)(2,1)} %param.7), channel_id=1, replica_groups=mesh['kv'=16,'head'=2] {'kv'}, dimensions={1}, use_global_device_ids=true | all-gather | bytes 278528 | tf_op jit(solution)/shard_map/all_gather | solution.py:34
  84.5 1.3 gather_fusion
  86.0 22.5 %fusion.2 = (f32[256,4,8]{2,1,0:T(4,128)S(1)}, f32[256,4,8,128]{3,2,1,0:T(8,128)}) fusion(pred[256,128]{1,0:T(8,128)(4,1)S(1)} %add_compare_fusion, bf16[256,4,128,128]{3,2,1,0:T(8,128)(2,1)} %param.8, bf16[256,4,8,128]{3,2,1,0:T(8,128)(2,1)S(1)} %gather_fusion), kind=kOutput, calls=%fused_computation.9 | convolution fusion | flops 271572992 | bytes 39911424 | tf_op jit(solution)/shard_map/gpqd,pgtd->pgqt/dot_general | solution.py:58
  109.0 1.0 gather_fusion.1
  110.0 8.4 %fusion.3 = f32[256,4,8]{2,1,0:T(4,128)S(1)} fusion(f32[256,4,8,128]{3,2,1,0:T(8,128)} %get-tuple-element.47, f32[256,4,8]{2,1,0:T(4,128)S(1)} %get-tuple-element.46, pred[256,128]{1,0:T(8,128)(4,1)S(1)} %add_compare_fusion), kind=kLoop, calls=%fused_computation.10 | loop fusion | flops 5234688 | bytes 4292608 | tf_op jit(solution)/shard_map/reduce_sum | solution.py:66
  118.6 0.5 convolution_bitcast_fusion
  119.1 0.8 copy.75
  119.9 3.7 %all-to-all-start.2 = ((f32[1,4,256]{1,0,2:T(1,128)}), f32[1,4,256]{1,0,2:T(1,128)S(1)}, u32[]{:S(2)}, u32[]{:S(2)}) async-start(f32[1,4,256]{1,0,2:T(1,128)} %bitcast.51), calls=%async_computation.2 | async-start | bytes 262144 | tf_op jit(solution)/shard_map/all_to_all | solution.py:87
  123.6 17.7 %broadcast_multiply_fusion = f32[256,4,8,128]{3,2,1,0:T(8,128)} fusion(f32[256,4,8]{2,1,0:T(4,128)S(1)} %bitcast.108, bf16[256,4,128,128]{3,2,1,0:T(8,128)(2,1)} %param.9, f32[256,4,8,128]{3,2,1,0:T(8,128)} %get-tuple-element.47, f32[256,4,8]{2,1,0:T(4,128)S(1)} %get-tuple-element.46, pred[256,128]{1,0:T(8,128)(4,1)S(1)} %add_compare_fusion), kind=kOutput, calls=%fused_computation.15 | convolution fusion | flops 274726912 | bytes 42041344 | tf_op jit(solution)/shard_map/pgqt,pgtd->pgqd/dot_general | solution.py:67
  141.4 0.9 copy.74
  142.3 6.7 %all-to-all-start.1 = ((f32[1,4,256]{1,0,2:T(1,128)}), f32[1,4,256]{1,0,2:T(1,128)S(1)}, u32[]{:S(2)}, u32[]{:S(2)}) async-start(f32[1,4,256]{1,0,2:T(1,128)} %bitcast.42), calls=%async_computation.1 | async-start | bytes 262144 | tf_op jit(solution)/shard_map/all_to_all | solution.py:86
  149.0 5.9 %fusion.16 = f32[4,32,8,128]{3,1,2,0:T(8,128)S(1)} fusion(f32[256,4,8,128]{3,2,1,0:T(8,128)} %broadcast_multiply_fusion, s32[256]{0:T(256)S(1)} %get-tuple-element.13), kind=kOutput, calls=%fused_computation.21 | convolution fusion | flops 402661376 | bytes 4719616 | tf_op jit(solution)/shard_map/sp,pgqd->gsqd/dot_general | solution.py:78
  155.2 1.1 copy.57
  156.3 0.5 all-to-all-done.1
  156.8 6.4 %all-to-all-start = ((f32[1,4,256,128]{3,1,0,2:T(4,128)}), f32[1,4,256,128]{3,1,0,2:T(4,128)S(1)}, u32[]{:S(2)}, u32[]{:S(2)}) async-start(f32[1,4,256,128]{3,1,0,2:T(4,128)} %copy.57), calls=%async_computation | async-start | bytes 1048576 | tf_op jit(solution)/shard_map/all_to_all | solution.py:88
  163.3 0.6 gather_fusion.2
  164.1 0.6 gather_fusion.3
  165.3 8.7 %all-to-all-done = f32[1,4,256,128]{3,1,0,2:T(4,128)S(1)} async-done(((f32[1,4,256,128]{3,1,0,2:T(4,128)}), f32[1,4,256,128]{3,1,0,2:T(4,128)S(1)}, u32[]{:S(2)}, u32[]{:S(2)}) %all-to-all-start) | async-done | bytes 524320 | tf_op jit(solution)/shard_map/all_to_all | solution.py:88
  174.3 0.6 copy.72
  (31 shorter events, 2.3 us)
Async XLA Ops:
  0.0 163.3 %copy-start = (bf16[32,4,128]{2,1,0:T(4,128)(2,1)S(1)}, bf16[32,4,128]{2,1,0:T(4,128)(2,1)}, u32[]{:S(2)}) copy-start(bf16[32,4,128]{2,1,0:T(4,128)(2,1)} %param.10) | copy-start | bytes 98308
  119.9 22.4 %all-to-all-start.2 = ((f32[1,4,256]{1,0,2:T(1,128)}), f32[1,4,256]{1,0,2:T(1,128)S(1)}, u32[]{:S(2)}, u32[]{:S(2)}) async-start(f32[1,4,256]{1,0,2:T(1,128)} %bitcast.51), calls=%async_computation.2 | async-start | bytes 262144 | tf_op jit(solution)/shard_map/all_to_all | solution.py:87
  141.4 22.5 %copy-start.1 = (bf16[4,16,128]{2,1,0:T(8,128)(2,1)S(1)}, bf16[4,16,128]{2,1,0:T(8,128)(2,1)}, u32[]{:S(2)}) copy-start(bf16[4,16,128]{2,1,0:T(8,128)(2,1)} %param.7) | copy-start | bytes 49156
  141.4 22.7 %copy-start.2 = (bf16[32,4,128]{2,1,0:T(4,128)(2,1)S(1)}, bf16[32,4,128]{2,1,0:T(4,128)(2,1)}, u32[]{:S(2)}) copy-start(bf16[32,4,128]{2,1,0:T(4,128)(2,1)} %param.11) | copy-start | bytes 98308
  142.3 14.5 %all-to-all-start.1 = ((f32[1,4,256]{1,0,2:T(1,128)}), f32[1,4,256]{1,0,2:T(1,128)S(1)}, u32[]{:S(2)}, u32[]{:S(2)}) async-start(f32[1,4,256]{1,0,2:T(1,128)} %bitcast.42), calls=%async_computation.1 | async-start | bytes 262144 | tf_op jit(solution)/shard_map/all_to_all | solution.py:86
  156.8 17.2 %all-to-all-start = ((f32[1,4,256,128]{3,1,0,2:T(4,128)}), f32[1,4,256,128]{3,1,0,2:T(4,128)S(1)}, u32[]{:S(2)}, u32[]{:S(2)}) async-start(f32[1,4,256,128]{3,1,0,2:T(4,128)} %copy.57), calls=%async_computation | async-start | bytes 1048576 | tf_op jit(solution)/shard_map/all_to_all | solution.py:88
where the time goes:
time: 176 us; the launch traced here: 175 us
  matrix products  46.7 us (27%)
  blocking collectives  44 us (25%)
  other arithmetic  30.5 us (17%)
  local copies, waits for them, and re-layouts  27.6 us (16%)
  starting transfers between devices  16.8 us (10%)
  waiting for transfers between devices  9.15 us (5%)
    all_gather x1, blocking collectives, on_device(): all_query = lax.all_gather(queries, 'kv', axis=1, tiled=True)  44 us
    dot_general x1, matrix products, on_device(): jnp.einsum('gpqd,pgtd->pgqt', page_query, key_cache, preferred_element_ty...  22.5 us
    sub x1, other arithmetic, on_device(): in_cache = (positions < (lengths[page_seq] - 1)[:, None])[:, None, None, :]  20.1 us
    dot_general x1, matrix products, on_device(): jnp.einsum('pgqt,pgtd->pgqd', weights.astype(jnp.bfloat16), value_cache,...  17.7 us
    scatter x1, local copies, waits for them, and re-layouts, on_device(): inverse = jnp.zeros((page_total,), jnp.int32).at[page_table].set(jnp.aran...  15.5 us
    all_to_all x1, waiting for transfers between devices, on_device(): lax.all_to_all(seq_out[None], 'kv', split_axis=2, concat_axis=0, tiled=True)  8.68 us
    reduce_sum x1, other arithmetic, on_device(): page_sum = jnp.sum(weights, axis=3)  8.45 us
    all_to_all x1, starting transfers between devices, on_device(): lax.all_to_all(seq_max[None], 'kv', split_axis=2, concat_axis=0, tiled=True)  6.69 us
  transfers between devices with their start and end apart: 3, of which 2 were waited for; matrix products, arithmetic and copies ran while one was open for 16% of the time, Pallas kernels for 0%

commit v1 on v0

--- a/solution.py
+++ b/solution.py
@@ -85,7 +85,12 @@
         (
             lax.all_to_all(seq_max[None], "kv", split_axis=2, concat_axis=0, tiled=True),
             lax.all_to_all(seq_sum[None], "kv", split_axis=2, concat_axis=0, tiled=True),
-            lax.all_to_all(seq_out[None], "kv", split_axis=2, concat_axis=0, tiled=True),
+            jnp.concatenate(
+                lax.all_to_all(
+                    jnp.stack(jnp.split(seq_out[None], lax.axis_size("kv"), axis=2)), "kv", 0, 0
+                ),
+                axis=0,
+            ),
         )
     )
     row_seq = (kv_index * local_rows + jnp.arange(local_rows, dtype=jnp.int32)) // group_size

time: 176 us -> 188 us (1.068)
  local copies, waits for them, and re-layouts: 27.6 us -> 36.1 us
  waiting for transfers between devices: 9.15 us -> 15.9 us
  starting transfers between devices: 16.8 us -> 14 us
    unnamed x6 -> x21, local copies, waits for them, and re-layouts: 0.01 us -> 9.08 us
    all_to_all x1, waiting for transfers between devices: 0.47 us -> 7.3 us  [on_device(): lax.all_to_all(seq_max[None], 'kv', split_axis=2, concat_axis=0, tiled=True)]
    all_to_all x1, starting transfers between devices: 6.44 us -> 3.57 us  [on_device(): lax.all_to_all(jnp.stack(jnp.split(seq_out[None], lax.axis_size('kv'), ax...]
  transfers between devices with their start and end apart: 3 -> 3, of which waited for: 2 -> 2; matrix products, arithmetic and copies ran while one was open for 16% -> 20% of each run, Pallas kernels for 0% -> 0%
where the time goes in v1:
time: 188 us; the launch traced here: 187 us
  matrix products  46.8 us (25%)
  blocking collectives  44 us (23%)
  local copies, waits for them, and re-layouts  36.1 us (19%)
  other arithmetic  30.5 us (16%)
  waiting for transfers between devices  15.9 us (8%)
  starting transfers between devices  14 us (7%)
    all_gather x1, blocking collectives, on_device(): all_query = lax.all_gather(queries, 'kv', axis=1, tiled=True)  44 us
    dot_general x1, matrix products, on_device(): jnp.einsum('gpqd,pgtd->pgqt', page_query, key_cache, preferred_element_ty...  22.5 us
    sub x1, other arithmetic, on_device(): in_cache = (positions < (lengths[page_seq] - 1)[:, None])[:, None, None, :]  20.1 us
    dot_general x1, matrix products, on_device(): jnp.einsum('pgqt,pgtd->pgqd', weights.astype(jnp.bfloat16), value_cache,...  17.8 us
    scatter x1, local copies, waits for them, and re-layouts, on_device(): inverse = jnp.zeros((page_total,), jnp.int32).at[page_table].set(jnp.aran...  15.5 us
    unnamed x21, local copies, waits for them, and re-layouts  9.08 us
    all_to_all x1, waiting for transfers between devices, on_device(): lax.all_to_all(jnp.stack(jnp.split(seq_out[None], lax.axis_size('kv'), ax...  8.62 us
    reduce_sum x1, other arithmetic, on_device(): page_sum = jnp.sum(weights, axis=3)  8.45 us
  transfers between devices with their start and end apart: 3, of which 2 were waited for; matrix products, arithmetic and copies ran while one was open for 20% of the time, Pallas kernels for 0%

profile of v1, /device:TPU:0, one launch (start us, length us, event | category | flops | bytes accessed | tf_op | source)
XLA Modules:
  0.0 187.5 jit_solution(9169428817913725714)
XLA Ops:
  0.0 2.1 %fusion.61 = (s32[1]{0:T(128)}, s32[1]{0:T(128)}, s32[1]{0:T(128)}, s32[1]{0:T(128)}, s32[1]{0:T(128)}, /*index=5*/s32[1]{0:T(128)}, s32[1]{0:T(128)}, s32[1]{0:...) fusion(s32[32]{0:T(128)} %param.12), kind=kLoop, calls=%fused_computation.140 | loop fusion | bytes 152 | tf_op jit(solution)/shard_map/gather | solution.py:62
  2.1 1.8 fusion.62
  3.9 0.7 compare_select_fusion
  4.7 15.5 %scatter_custom_fusion = s32[4096]{0:T(1024)S(1)} fusion(s32[4096]{0:T(1024)S(1)} %compare_select_fusion, s32[4096]{0:T(1024)S(1)} %iota.23, s32[]{:T(128)} %constant.32.clone.1), kind=kCustom, calls=%fused_computation.80 | custom fusion | bytes 16388 | tf_op jit(solution)/shard_map/scatter | solution.py:50
  20.3 20.1 %fusion.52 = (s32[256]{0:T(256)S(1)}, s32[256]{0:T(256)S(1)}) fusion(s32[]{:T(128)} %bitcast, s32[]{:T(128)} %bitcast.1, s32[]{:T(128)} %bitcast.2, s32[]{:T(128)} %bitcast.3, s32[]{:T(128)} %bitcast.4, s32[]{:T(128)} %bitcast.5, s32[]{:T(128)} %bitcast.6, s32[]{:T(128)} %bitcast.7, s32[]{:T(128)} %bitcast.8, s32[]{:T(128)} %bitcast.9, s32[]{:T(128)} %bitcast.10, ...), kind=kLoop, calls=%fused_computation.132 | loop fusion | flops 20736 | bytes 3204 | tf_op jit(solution)/shard_map/sub | solution.py:62
  40.5 44.0 %all_gather.3 = bf16[4,256,128]{2,1,0:T(8,128)(2,1)S(1)} all-gather(bf16[4,16,128]{2,1,0:T(8,128)(2,1)} %param.7), channel_id=1, replica_groups=mesh['kv'=16,'head'=2] {'kv'}, dimensions={1}, use_global_device_ids=true | all-gather | bytes 278528 | tf_op jit(solution)/shard_map/all_gather | solution.py:34
  84.5 1.3 gather_fusion
  86.0 22.5 %fusion.2 = (f32[256,4,8]{2,1,0:T(4,128)S(1)}, f32[256,4,8,128]{3,2,1,0:T(8,128)}) fusion(pred[256,128]{1,0:T(8,128)(4,1)S(1)} %add_compare_fusion, bf16[256,4,128,128]{3,2,1,0:T(8,128)(2,1)} %param.8, bf16[256,4,8,128]{3,2,1,0:T(8,128)(2,1)S(1)} %gather_fusion), kind=kOutput, calls=%fused_computation.9 | convolution fusion | flops 271572992 | bytes 39911424 | tf_op jit(solution)/shard_map/gpqd,pgtd->pgqt/dot_general | solution.py:58
  109.0 1.0 gather_fusion.1
  110.0 8.4 %fusion.3 = f32[256,4,8]{2,1,0:T(4,128)S(1)} fusion(f32[256,4,8,128]{3,2,1,0:T(8,128)} %get-tuple-element.47, f32[256,4,8]{2,1,0:T(4,128)S(1)} %get-tuple-element.46, pred[256,128]{1,0:T(8,128)(4,1)S(1)} %add_compare_fusion), kind=kLoop, calls=%fused_computation.10 | loop fusion | flops 5234688 | bytes 4292608 | tf_op jit(solution)/shard_map/reduce_sum | solution.py:66
  119.1 0.8 copy.74
  119.9 3.7 %all-to-all-start.2 = ((f32[1,4,256]{1,0,2:T(1,128)}), f32[1,4,256]{1,0,2:T(1,128)S(1)}, u32[]{:S(2)}, u32[]{:S(2)}) async-start(f32[1,4,256]{1,0,2:T(1,128)} %bitcast.65), calls=%async_computation.2 | async-start | bytes 262144 | tf_op jit(solution)/shard_map/all_to_all | solution.py:87
  123.6 17.8 %broadcast_multiply_fusion = f32[256,4,8,128]{3,2,1,0:T(8,128)} fusion(f32[256,4,8]{2,1,0:T(4,128)S(1)} %bitcast.183, bf16[256,4,128,128]{3,2,1,0:T(8,128)(2,1)} %param.9, f32[256,4,8,128]{3,2,1,0:T(8,128)} %get-tuple-element.47, f32[256,4,8]{2,1,0:T(4,128)S(1)} %get-tuple-element.46, pred[256,128]{1,0:T(8,128)(4,1)S(1)} %add_compare_fusion), kind=kOutput, calls=%fused_computation.15 | convolution fusion | flops 274726912 | bytes 42041344 | tf_op jit(solution)/shard_map/pgqt,pgtd->pgqd/dot_general | solution.py:67
  141.4 5.9 %fusion.16 = f32[4,32,8,128]{3,1,2,0:T(8,128)S(1)} fusion(f32[256,4,8,128]{3,2,1,0:T(8,128)} %broadcast_multiply_fusion, s32[256]{0:T(256)S(1)} %get-tuple-element.13), kind=kOutput, calls=%fused_computation.21 | convolution fusion | flops 402661376 | bytes 4719616 | tf_op jit(solution)/shard_map/sp,pgqd->gsqd/dot_general | solution.py:78
  150.7 0.6 fusion.31
  151.9 0.6 fusion.29
  153.7 0.6 fusion.26
  154.3 0.6 fusion.25
  156.7 0.9 copy.72
  157.6 6.7 %all-to-all-start.1 = ((f32[1,4,256]{1,0,2:T(1,128)}), f32[1,4,256]{1,0,2:T(1,128)S(1)}, u32[]{:S(2)}, u32[]{:S(2)}) async-start(f32[1,4,256]{1,0,2:T(1,128)} %bitcast.56), calls=%async_computation.1 | async-start | bytes 262144 | tf_op jit(solution)/shard_map/all_to_all | solution.py:86
  164.9 7.3 %all-to-all-done.1 = f32[1,4,256]{1,0,2:T(1,128)S(1)} async-done(((f32[1,4,256]{1,0,2:T(1,128)}), f32[1,4,256]{1,0,2:T(1,128)S(1)}, u32[]{:S(2)}, u32[]{:S(2)}) %all-to-all-start.1) | async-done | bytes 4128 | tf_op jit(solution)/shard_map/all_to_all | solution.py:86
  172.2 3.6 %all-to-all-start = ((f32[16,1,4,16,128]{4,3,2,1,0:T(8,128)}), f32[16,1,4,16,128]{4,3,2,1,0:T(8,128)S(1)}, u32[]{:S(2)}, u32[]{:S(2)}) async-start(f32[16,1,4,16,128]{4,3,2,1,0:T(8,128)} %fusion.21), calls=%async_computation | async-start | bytes 1048576 | tf_op jit(solution)/shard_map/all_to_all | solution.py:89
  177.9 8.6 %all-to-all-done = f32[16,1,4,16,128]{4,3,2,1,0:T(8,128)S(1)} async-done(((f32[16,1,4,16,128]{4,3,2,1,0:T(8,128)}), f32[16,1,4,16,128]{4,3,2,1,0:T(8,128)S(1)}, u32[]{:S(2)}, u32[]{:S(2)}) %all-to-all-start) | async-done | bytes 524320 | tf_op jit(solution)/shard_map/all_to_all | solution.py:89
  186.9 0.6 copy.70
  (47 shorter events, 11.3 us)
Async XLA Ops:
  0.0 175.9 %copy-start = (bf16[32,4,128]{2,1,0:T(4,128)(2,1)S(1)}, bf16[32,4,128]{2,1,0:T(4,128)(2,1)}, u32[]{:S(2)}) copy-start(bf16[32,4,128]{2,1,0:T(4,128)(2,1)} %param.10) | copy-start | bytes 98308
  119.9 37.7 %all-to-all-start.2 = ((f32[1,4,256]{1,0,2:T(1,128)}), f32[1,4,256]{1,0,2:T(1,128)S(1)}, u32[]{:S(2)}, u32[]{:S(2)}) async-start(f32[1,4,256]{1,0,2:T(1,128)} %bitcast.65), calls=%async_computation.2 | async-start | bytes 262144 | tf_op jit(solution)/shard_map/all_to_all | solution.py:87
  141.4 35.0 %copy-start.1 = (bf16[4,16,128]{2,1,0:T(8,128)(2,1)S(1)}, bf16[4,16,128]{2,1,0:T(8,128)(2,1)}, u32[]{:S(2)}) copy-start(bf16[4,16,128]{2,1,0:T(8,128)(2,1)} %param.7) | copy-start | bytes 49156
  141.4 35.2 %copy-start.2 = (bf16[32,4,128]{2,1,0:T(4,128)(2,1)S(1)}, bf16[32,4,128]{2,1,0:T(4,128)(2,1)}, u32[]{:S(2)}) copy-start(bf16[32,4,128]{2,1,0:T(4,128)(2,1)} %param.11) | copy-start | bytes 98308
  157.6 14.6 %all-to-all-start.1 = ((f32[1,4,256]{1,0,2:T(1,128)}), f32[1,4,256]{1,0,2:T(1,128)S(1)}, u32[]{:S(2)}, u32[]{:S(2)}) async-start(f32[1,4,256]{1,0,2:T(1,128)} %bitcast.56), calls=%async_computation.1 | async-start | bytes 262144 | tf_op jit(solution)/shard_map/all_to_all | solution.py:86
  172.2 14.3 %all-to-all-start = ((f32[16,1,4,16,128]{4,3,2,1,0:T(8,128)}), f32[16,1,4,16,128]{4,3,2,1,0:T(8,128)S(1)}, u32[]{:S(2)}, u32[]{:S(2)}) async-start(f32[16,1,4,16,128]{4,3,2,1,0:T(8,128)} %fusion.21), calls=%async_computation | async-start | bytes 1048576 | tf_op jit(solution)/shard_map/all_to_all | solution.py:89
